TPU v7x, 32 devices: a whole 2x2x4 slice. The times are simulated.
32 devices in a mesh: section: 2 (over core), dp: 8 (over z, x), mp: 2 (over y).
Axes of the slice: x: 2, y: 2, z: 4, core: 2. Of those that a mesh axis runs over, the one named last changes fastest.
Arguments:
- images: bfloat16 [2, 16, 197, 1024], P(None, 'dp'), may hold values from -6 to 6
- cotangent: bfloat16 [2, 16, 197, 1024], P(None, 'dp'), may hold values from -6 to 6
- live_count: int32 [2, 8], P(None, 'dp'), may hold values from 1 to 2, as said below
- ln1_gain: bfloat16 [2, 1024], P('section', 'dp'), may hold values from 0.099609375 to 1.8984375
- ln1_bias: bfloat16 [2, 1024], P('section', 'dp'), may hold values from -3 to 3
- qkv_weight: bfloat16 [2, 3, 1024, 1024], P('section', None, 'dp', 'mp'), may hold values from -0.1875 to 0.1875
- qv_bias: bfloat16 [2, 2, 16, 64], P('section', None, 'mp', 'dp'), may hold values from -3 to 3
- out_weight: bfloat16 [2, 1024, 1024], P('section', 'mp', 'dp'), may hold values from -1.5 to 1.5
- out_bias: bfloat16 [2, 1024], P('section', 'dp'), may hold values from -3 to 3
- ln2_gain: bfloat16 [2, 1024], P('section', 'dp'), may hold values from 0.099609375 to 1.8984375
- ln2_bias: bfloat16 [2, 1024], P('section', 'dp'), may hold values from -3 to 3
- up_weight: bfloat16 [2, 1024, 4096], P('section', 'dp', 'mp'), may hold values from -0.1875 to 0.1875
- up_bias: bfloat16 [2, 16, 256], P('section', 'mp', 'dp'), may hold values from -3 to 3
- down_weight: bfloat16 [2, 4096, 1024], P('section', 'mp', 'dp'), may hold values from -0.09375 to 0.09375
- down_bias: bfloat16 [2, 1024], P('section', 'dp'), may hold values from -3 to 3
Outputs:
- activations: bfloat16 [2, 2, 16, 197, 1024], P('section', None, 'dp')
- input_grads: bfloat16 [2, 2, 16, 197, 1024], P('section', None, 'dp')
- grad_ln1_gain: float32 [2, 1024], P('section', 'dp')
- grad_ln1_bias: float32 [2, 1024], P('section', 'dp')
- grad_qkv_weight: float32 [2, 3, 1024, 1024], P('section', None, 'dp', 'mp')
- grad_qv_bias: float32 [2, 2, 16, 64], P('section', None, 'mp', 'dp')
- grad_out_weight: float32 [2, 1024, 1024], P('section', 'mp', 'dp')
- grad_out_bias: float32 [2, 1024], P('section', 'dp')
- grad_ln2_gain: float32 [2, 1024], P('section', 'dp')
- grad_ln2_bias: float32 [2, 1024], P('section', 'dp')
- grad_up_weight: float32 [2, 1024, 4096], P('section', 'dp', 'mp')
- grad_up_bias: float32 [2, 16, 256], P('section', 'mp', 'dp')
- grad_down_weight: float32 [2, 4096, 1024], P('section', 'mp', 'dp')
- grad_down_bias: float32 [2, 1024], P('section', 'dp')
Inputs may be any that keep to these rules, and one draw needn't show every extreme that they name: Micro-batch m has live_count[m, d] images on data device d, in its first slots; its other slots hold values that no output reads.
All inputs are finite; a program needn't handle non-finite values.
Results may differ from a plain program's by a relative error of at most 0.015.
Values may be sent and summed in bfloat16 or wider, within the bound.
A program may use at most 256 MiB of HBM per device.

v0:
```python
import math
import jax
import jax.numpy as jnp
from jax import lax
from jax.sharding import PartitionSpec as P

HD = 64
epsilon = 1e-06


def gather_all(small, big):
    flat = jnp.concatenate([piece.reshape(-1) for piece in small])
    packed = lax.all_gather(flat, "dp", axis=0, tiled=False)
    count = packed.shape[0]
    whole, offset = ([], 0)
    for piece, axis in zip(small, (1, 1, 3, 1, 1, 1, 2, 1)):
        part = packed[:, offset : offset + piece.size].reshape((count,) + piece.shape)
        offset += piece.size
        part = jnp.moveaxis(part, 0, axis)
        shape = list(piece.shape)
        shape[axis] *= count
        whole.append(part.reshape(shape))
    qkv, out, up, down = (
        lax.all_gather(piece, "dp", axis=axis, tiled=True) for piece, axis in zip(big, (2, 2, 1, 2))
    )
    return (
        whole[0],
        whole[1],
        qkv,
        whole[2],
        out,
        whole[3],
        whole[4],
        whole[5],
        up,
        whole[6],
        down,
        whole[7],
    )


def scatter_all(totals, shards):
    small_at = (0, 1, 3, 5, 6, 7, 9, 11)
    count = lax.axis_size("dp")
    rows = []
    for index, axis in zip(small_at, (1, 1, 3, 1, 1, 1, 2, 1)):
        piece = totals[index]
        shape = list(piece.shape)
        shape[axis : axis + 1] = [count, shape[axis] // count]
        rows.append(jnp.moveaxis(piece.reshape(shape), axis, 0).reshape(count, -1))
    packed = lax.psum_scatter(jnp.concatenate(rows, axis=1), "dp", scatter_dimension=0, tiled=False)
    owned, offset = ([None] * 12, 0)
    for index in small_at:
        size = shards[index].size
        owned[index] = packed[offset : offset + size].reshape(shards[index].shape)
        offset += size
    for index, axis in zip((2, 4, 8, 10), (2, 2, 1, 2)):
        owned[index] = lax.psum_scatter(
            totals[index].astype(jnp.bfloat16), "dp", scatter_dimension=axis, tiled=True
        ).astype(jnp.float32)
    return owned


def both_halves(partial):
    return lax.psum(partial.astype(jnp.bfloat16), "mp").astype(jnp.float32)


def from_behind(x, axis, by):
    length = lax.axis_size(axis)
    pairs = [(i, i + by) for i in range(length) if 0 <= i + by < length]
    return lax.ppermute(x, axis, pairs)


def norm_parts(stream):
    centered = stream - jnp.mean(stream, axis=-1, keepdims=True)
    inverse = lax.rsqrt(jnp.mean(centered * centered, axis=-1, keepdims=True) + epsilon)
    return (centered * inverse, inverse)


def norm_back(grad_normed, normed, inverse):
    first_mean = jnp.mean(grad_normed, axis=-1, keepdims=True)
    second_mean = jnp.mean(grad_normed * normed, axis=-1, keepdims=True)
    return inverse * (grad_normed - first_mean - normed * second_mean)


def gelu_slope(preact):
    cumul = 0.5 * (1.0 + lax.erf(preact * 2.0 ** (-0.5)))
    density = jnp.exp(-0.5 * preact * preact) * (2.0 * math.pi) ** (-0.5)
    return cumul + preact * density


def unpack_weights(whole):
    return (
        whole[0][0].astype(jnp.float32),
        whole[1][0].astype(jnp.float32),
        whole[2][0],
        whole[3][0].reshape(2, -1).astype(jnp.float32),
        whole[4][0],
        whole[5][0].astype(jnp.float32),
        whole[6][0].astype(jnp.float32),
        whole[7][0].astype(jnp.float32),
        whole[8][0],
        whole[9][0].reshape(-1).astype(jnp.float32),
        whole[10][0],
        whole[11][0].astype(jnp.float32),
    )


def forward(stream, params, rows):
    (
        gain_one,
        shift_one,
        qkv_mat,
        qv_shift,
        out_mat,
        out_shift,
        gain_two,
        shift_two,
        up_mat,
        up_shift,
        down_mat,
        down_shift,
    ) = params
    batch_size, seq_len, model_width = stream.shape
    head_count = qkv_mat.shape[2] // HD
    scale = HD ** (-0.5)
    normed, inverse = norm_parts(stream)
    lowered = (normed * gain_one + shift_one).astype(jnp.bfloat16)
    projected = jnp.einsum("bld,cde->cble", lowered, qkv_mat, preferred_element_type=jnp.float32)
    split_shape = (batch_size, seq_len, head_count, HD)
    queries = (projected[0] + qv_shift[0]).astype(jnp.bfloat16).reshape(split_shape)
    keys_low = projected[1].astype(jnp.bfloat16).reshape(split_shape)
    values_low = (projected[2] + qv_shift[1]).astype(jnp.bfloat16).reshape(split_shape)
    scores = (
        jnp.einsum("blhe,bmhe->bhlm", queries, keys_low, preferred_element_type=jnp.float32) * scale
    )
    row_max = jnp.max(scores, axis=-1, keepdims=True)
    log_total = row_max + jnp.log(jnp.sum(jnp.exp(scores - row_max), axis=-1, keepdims=True))
    attn_probs = jnp.exp(scores - log_total)
    mixed = jnp.einsum(
        "bhlm,bmhe->blhe",
        attn_probs.astype(jnp.bfloat16),
        values_low,
        preferred_element_type=jnp.float32,
    )
    mixed = mixed.astype(jnp.bfloat16).reshape(batch_size, seq_len, -1)
    partial_attn = jnp.einsum("bld,de->ble", mixed, out_mat, preferred_element_type=jnp.float32)
    middle = stream + both_halves(partial_attn) + out_shift
    normed_two, inverse_two = norm_parts(middle)
    lowered_two = (normed_two * gain_two + shift_two).astype(jnp.bfloat16)
    preact = (
        jnp.einsum("bld,df->blf", lowered_two, up_mat, preferred_element_type=jnp.float32)
        + up_shift
    )
    gelu_out = jax.nn.gelu(preact, approximate=False).astype(jnp.bfloat16)
    partial_mlp = jnp.einsum("blf,fd->bld", gelu_out, down_mat, preferred_element_type=jnp.float32)
    result = (middle + both_halves(partial_mlp) + down_shift) * rows
    return (result, (stream, middle, queries, keys_low, values_low, log_total, mixed, preact))


def backward(seed, saved, params, shapes):
    (
        gain_one,
        shift_one,
        qkv_mat,
        qv_shift,
        out_mat,
        out_shift,
        gain_two,
        shift_two,
        up_mat,
        up_shift,
        down_mat,
        down_shift,
    ) = params
    stream, middle, queries, keys_low, values_low, log_total, mixed, preact = saved
    batch_size, seq_len, head_count, head_dim = queries.shape
    scale = HD ** (-0.5)
    normed, inverse = norm_parts(stream)
    lowered = (normed * gain_one + shift_one).astype(jnp.bfloat16)
    normed_two, inverse_two = norm_parts(middle)
    lowered_two = (normed_two * gain_two + shift_two).astype(jnp.bfloat16)
    gelu_out = jax.nn.gelu(preact, approximate=False).astype(jnp.bfloat16)
    grad_mlp = seed.astype(jnp.bfloat16)
    grad_down_shift = jnp.sum(grad_mlp.astype(jnp.float32), axis=(0, 1))
    grad_down_mat = jnp.einsum(
        "blf,bld->fd", gelu_out, grad_mlp, preferred_element_type=jnp.float32
    )
    grad_gelu = jnp.einsum("bld,fd->blf", grad_mlp, down_mat, preferred_element_type=jnp.float32)
    grad_pre = (grad_gelu * gelu_slope(preact)).astype(jnp.bfloat16)
    grad_up_shift = jnp.sum(grad_pre.astype(jnp.float32), axis=(0, 1))
    grad_up_mat = jnp.einsum(
        "bld,blf->df", lowered_two, grad_pre, preferred_element_type=jnp.float32
    )
    grad_low_two = both_halves(
        jnp.einsum("blf,df->bld", grad_pre, up_mat, preferred_element_type=jnp.float32)
    )
    grad_gain_two = jnp.sum(grad_low_two * normed_two, axis=(0, 1))
    grad_shift_two = jnp.sum(grad_low_two, axis=(0, 1))
    grad_middle = seed + norm_back(grad_low_two * gain_two, normed_two, inverse_two)
    grad_attn = grad_middle.astype(jnp.bfloat16)
    grad_out_shift = jnp.sum(grad_attn.astype(jnp.float32), axis=(0, 1))
    grad_out_mat = jnp.einsum("bld,ble->de", mixed, grad_attn, preferred_element_type=jnp.float32)
    grad_mixed = jnp.einsum("ble,de->bld", grad_attn, out_mat, preferred_element_type=jnp.float32)
    grad_mixed = grad_mixed.astype(jnp.bfloat16).reshape(batch_size, seq_len, head_count, head_dim)
    scores = (
        jnp.einsum("blhe,bmhe->bhlm", queries, keys_low, preferred_element_type=jnp.float32) * scale
    )
    attn_probs = jnp.exp(scores - log_total)
    grad_probs = jnp.einsum(
        "blhe,bmhe->bhlm", grad_mixed, values_low, preferred_element_type=jnp.float32
    )
    grad_values = jnp.einsum(
        "bhlm,blhe->bmhe",
        attn_probs.astype(jnp.bfloat16),
        grad_mixed,
        preferred_element_type=jnp.float32,
    ).astype(jnp.bfloat16)
    grad_scores = (
        attn_probs * (grad_probs - jnp.sum(attn_probs * grad_probs, axis=-1, keepdims=True))
    ).astype(jnp.bfloat16)
    grad_queries = (
        jnp.einsum("bhlm,bmhe->blhe", grad_scores, keys_low, preferred_element_type=jnp.float32)
        * scale
    ).astype(jnp.bfloat16)
    grad_keys = (
        jnp.einsum("bhlm,blhe->bmhe", grad_scores, queries, preferred_element_type=jnp.float32)
        * scale
    ).astype(jnp.bfloat16)
    grad_proj = jnp.stack([grad_queries, grad_keys, grad_values]).reshape(
        3, batch_size, seq_len, -1
    )
    grad_qv_shift = jnp.stack(
        [
            jnp.sum(grad_queries.astype(jnp.float32), axis=(0, 1)),
            jnp.sum(grad_values.astype(jnp.float32), axis=(0, 1)),
        ]
    )
    grad_qkv_mat = jnp.einsum(
        "bld,cble->cde", lowered, grad_proj, preferred_element_type=jnp.float32
    )
    grad_lowered = both_halves(
        jnp.einsum("cble,cde->bld", grad_proj, qkv_mat, preferred_element_type=jnp.float32)
    )
    grad_gain_one = jnp.sum(grad_lowered * normed, axis=(0, 1))
    grad_shift_one = jnp.sum(grad_lowered, axis=(0, 1))
    grad_stream = grad_middle + norm_back(grad_lowered * gain_one, normed, inverse)
    terms = [
        grad_gain_one,
        grad_shift_one,
        grad_qkv_mat,
        grad_qv_shift,
        grad_out_mat,
        grad_out_shift,
        grad_gain_two,
        grad_shift_two,
        grad_up_mat,
        grad_up_shift,
        grad_down_mat,
        grad_down_shift,
    ]
    return (grad_stream, [term.reshape(shape) for term, shape in zip(terms, shapes)])


def local(
    images,
    cotangent,
    live_count,
    ln1_gain,
    ln1_bias,
    qkv_weight,
    qv_bias,
    out_weight,
    out_bias,
    ln2_gain,
    ln2_bias,
    up_weight,
    up_bias,
    down_weight,
    down_bias,
):
    first_section = lax.axis_index("section") == 0
    micro_count = images.shape[0]
    slot_count = images.shape[1]
    slot_ids = jnp.arange(slot_count)
    small = (ln1_gain, ln1_bias, qv_bias, out_bias, ln2_gain, ln2_bias, up_bias, down_bias)
    gathered = gather_all(small, (qkv_weight, out_weight, up_weight, down_weight))
    params = unpack_weights(gathered)
    shapes = [piece.shape for piece in gathered]

    def row_mask(batch_index, valid):
        alive = jnp.logical_and(slot_ids < live_count[batch_index, 0], valid)
        return alive.astype(jnp.float32).reshape(slot_count, 1, 1)

    def choose(for_first, for_second):
        return jnp.where(first_section, for_first, for_second)

    incoming = jnp.zeros(images.shape[1:], jnp.bfloat16)
    outputs = []
    kept = []
    for moment in range(micro_count + 1):
        own = images[min(moment, micro_count - 1)]
        source = choose(own, incoming).astype(jnp.float32)
        rows = choose(
            row_mask(min(moment, micro_count - 1), moment < micro_count),
            row_mask(max(moment - 1, 0), moment >= 1),
        )
        result, saved = forward(source, params, rows)
        result = result.astype(jnp.bfloat16)
        outputs.append(result)
        kept.append(saved)
        if moment < micro_count:
            incoming = from_behind(result, "section", 1)
    activations = jnp.stack(
        [choose(outputs[index], outputs[index + 1]) for index in range(micro_count)]
    )
    totals = [jnp.zeros(shape, jnp.float32) for shape in shapes]
    incoming = jnp.zeros(images.shape[1:], jnp.bfloat16)
    returned = []
    for moment in range(micro_count + 1):
        later_index = min(moment, micro_count - 1)
        rows = choose(
            row_mask(max(moment - 1, 0), moment >= 1), row_mask(later_index, moment < micro_count)
        )
        seed = choose(incoming, cotangent[later_index]).astype(jnp.float32) * rows
        saved = jax.tree.map(choose, kept[max(moment - 1, 0)], kept[min(moment + 1, micro_count)])
        grad_stream, terms = backward(seed, saved, params, shapes)
        grad_low = grad_stream.astype(jnp.bfloat16)
        returned.append(grad_low)
        if moment < micro_count:
            incoming = from_behind(grad_low, "section", -1)
        totals = [first_part + second_part for first_part, second_part in zip(totals, terms)]
    shards = (
        ln1_gain,
        ln1_bias,
        qkv_weight,
        qv_bias,
        out_weight,
        out_bias,
        ln2_gain,
        ln2_bias,
        up_weight,
        up_bias,
        down_weight,
        down_bias,
    )
    owned = scatter_all(totals, shards)
    input_grads = jnp.stack(
        [choose(returned[index + 1], returned[index]) for index in range(micro_count)]
    )
    return (
        activations[None],
        input_grads[None],
        owned[0],
        owned[1],
        owned[2],
        owned[3],
        owned[4],
        owned[5],
        owned[6],
        owned[7],
        owned[8],
        owned[9],
        owned[10],
        owned[11],
    )


def solution(mesh):
    return jax.shard_map(
        local,
        mesh=mesh,
        in_specs=(
            P(None, "dp", None, None),
            P(None, "dp", None, None),
            P(None, "dp"),
            P("section", "dp"),
            P("section", "dp"),
            P("section", None, "dp", "mp"),
            P("section", None, "mp", "dp"),
            P("section", "mp", "dp"),
            P("section", "dp"),
            P("section", "dp"),
            P("section", "dp"),
            P("section", "dp", "mp"),
            P("section", "mp", "dp"),
            P("section", "mp", "dp"),
            P("section", "dp"),
        ),
        out_specs=(
            P("section", None, "dp", None, None),
            P("section", None, "dp", None, None),
            P("section", "dp"),
            P("section", "dp"),
            P("section", None, "dp", "mp"),
            P("section", None, "mp", "dp"),
            P("section", "mp", "dp"),
            P("section", "dp"),
            P("section", "dp"),
            P("section", "dp"),
            P("section", "dp", "mp"),
            P("section", "mp", "dp"),
            P("section", "mp", "dp"),
            P("section", "dp"),
        ),
        check_vma=False,
    )
```

profile of v0, /device:TPU:0, one launch (start us, length us, event | category | flops | bytes accessed | tf_op | source)
XLA Modules:
  0.0 1204.3 jit_solution(4596555902169269443)
XLA Ops:
  15.5 32.9 %all-gather.1 = bf16[8,1,1152]{2,1,0:T(2,128)(2,1)S(1)} all-gather(bf16[1,1,1152]{2,1,0:T(2,128)(2,1)S(1)} %reshape.803), channel_id=2, replica_groups=mesh['section'=2,'dp'=8,'mp'=2] {'dp'}, dimensions={0}, use_global_device_ids=true | all-gather | bytes 20736 | tf_op jit(solution)/shard_map/all_gather | solution.py:13
  52.2 20.9 %all-gather.7.cloned.1.call-done = bf16[1,3,1024,512]{3,2,1,0:T(8,128)(2,1)} async-done(((bf16[1,3,128,512]{3,2,1,0:T(8,128)(2,1)}), bf16[1,3,1024,512]{3,2,1,0:T(8,128)(2,1)}) %all-gather.7.cloned.1.call-update) | async-done | bytes 3145744 | tf_op jit(solution)/shard_map/all_gather | solution.py:24
  87.2 26.0 %all-gather.9.cloned.1.call-done = bf16[1,512,1024]{2,1,0:T(8,128)(2,1)} async-done(((bf16[1,512,128]{2,1,0:T(8,128)(2,1)}), bf16[1,512,1024]{2,1,0:T(8,128)(2,1)}) %all-gather.9.cloned.1.call-update) | async-done | bytes 1048592 | tf_op jit(solution)/shard_map/all_gather | solution.py:24
  118.3 32.0 %all-reduce.14.cloned.1.call-done = bf16[2,197,1024]{2,1,0:T(8,128)(2,1)} async-done(((bf16[2,197,1024]{2,1,0:T(8,128)(2,1)}), bf16[2,197,1024]{2,1,0:T(8,128)(2,1)}) %all-reduce.14.cloned.1.call-update) | async-done | bytes 806928 | tf_op jit(solution)/shard_map/psum | solution.py:65
  153.7 71.4 %all-gather.11.cloned.1.call-done = bf16[1,1024,2048]{2,1,0:T(8,128)(2,1)} async-done(((bf16[1,128,2048]{2,1,0:T(8,128)(2,1)}), bf16[1,1024,2048]{2,1,0:T(8,128)(2,1)}) %all-gather.11.cloned.1.call-update) | async-done | bytes 4194320 | tf_op jit(solution)/shard_map/all_gather | solution.py:24
  225.1 7.2 fusion.571
  232.2 67.9 %all-gather.13.cloned.1.call-done = bf16[1,2048,1024]{2,1,0:T(8,128)(2,1)} async-done(((bf16[1,2048,128]{2,1,0:T(8,128)(2,1)}), bf16[1,2048,1024]{2,1,0:T(8,128)(2,1)}) %all-gather.13.cloned.1.call-update) | async-done | bytes 4194320 | tf_op jit(solution)/shard_map/all_gather | solution.py:24
  300.2 13.1 %fusion.460 = bf16[2,197,1024]{2,1,0:T(8,128)(2,1)} fusion(bf16[1,2048,1024]{2,1,0:T(8,128)(2,1)} %all-gather.13.cloned.1.call-done, f32[2,197,2048]{2,1,0:T(8,128)} %get-tuple-element.200, u8[197,2048]{1,0:T(8,128)(4,1)S(1)} %get-tuple-element.75, u8[197,2048]{1,0:T(8,128)(4,1)S(1)} %get-tuple-element.74), kind=kOutput, calls=%fused_computation.599 | convolution fusion | flops 1709443072 | bytes 9035776 | tf_op jit(solution)/shard_map/blf,fd->bld/dot_general | solution.py:156
  314.6 32.1 %all-reduce.16.cloned.1.call-done = bf16[2,197,1024]{2,1,0:T(8,128)(2,1)} async-done(((bf16[2,197,1024]{2,1,0:T(8,128)(2,1)}), bf16[2,197,1024]{2,1,0:T(8,128)(2,1)}) %all-reduce.16.cloned.1.call-update) | async-done | bytes 806928 | tf_op jit(solution)/shard_map/psum | solution.py:65
  372.0 32.1 %all-reduce.18.cloned.1.call-done = bf16[2,197,1024]{2,1,0:T(8,128)(2,1)} async-done(((bf16[2,197,1024]{2,1,0:T(8,128)(2,1)}), bf16[2,197,1024]{2,1,0:T(8,128)(2,1)}) %all-reduce.18.cloned.1.call-update) | async-done | bytes 806928 | tf_op jit(solution)/shard_map/psum | solution.py:65
  409.2 7.5 fusion.568
  424.0 11.5 fusion.465
  441.0 47.7 %all-reduce.30.cloned.1.call-done = (bf16[2,197,1024]{2,1,0:T(8,128)(2,1)}, bf16[2,197,1024]{2,1,0:T(8,128)(2,1)}) async-done(((bf16[2,197,1024]{2,1,0:T(8,128)(2,1)}, bf16[2,197,1024]{2,1,0:T(8,128)(2,1)}), (bf16[2,197,1024]{2,1,0:T(8,128)(2,1)}, bf16[2,197,1024]{2,1,0:T(8,128)(2,1)})) %all-reduce.30.cloned.1.call-update) | async-done | bytes 1613840 | tf_op jit(solution)/shard_map/psum | solution.py:65
  546.8 47.9 %all-reduce.28.cloned.1.call-done = (bf16[2,197,1024]{2,1,0:T(8,128)(2,1)}, bf16[2,197,1024]{2,1,0:T(8,128)(2,1)}) async-done(((bf16[2,197,1024]{2,1,0:T(8,128)(2,1)}, bf16[2,197,1024]{2,1,0:T(8,128)(2,1)}), (bf16[2,197,1024]{2,1,0:T(8,128)(2,1)}, bf16[2,197,1024]{2,1,0:T(8,128)(2,1)})) %all-reduce.28.cloned.1.call-update) | async-done | bytes 1613840 | tf_op jit(solution)/shard_map/psum | solution.py:65
  596.2 5.4 fusion.834
  605.4 10.2 fusion.569
  628.1 33.2 %all-reduce.20.cloned.1.call-done = bf16[2,197,1024]{2,1,0:T(8,128)(2,1)} async-done(((bf16[2,197,1024]{2,1,0:T(8,128)(2,1)}), bf16[2,197,1024]{2,1,0:T(8,128)(2,1)}) %all-reduce.20.cloned.1.call-update) | async-done | bytes 806928 | tf_op jit(solution)/shard_map/psum | solution.py:65
  693.6 35.2 %all-reduce.22.cloned.1.call-done = bf16[2,197,1024]{2,1,0:T(8,128)(2,1)} async-done(((bf16[2,197,1024]{2,1,0:T(8,128)(2,1)}), bf16[2,197,1024]{2,1,0:T(8,128)(2,1)}) %all-reduce.22.cloned.1.call-update) | async-done | bytes 806928 | tf_op jit(solution)/shard_map/psum | solution.py:65
  749.7 13.1 %fusion.470 = bf16[2,197,1024]{2,1,0:T(8,128)(2,1)} fusion(bf16[1,2048,1024]{2,1,0:T(8,128)(2,1)} %all-gather.13.cloned.1.call-done, f32[2,197,2048]{2,1,0:T(8,128)} %get-tuple-element.208, u8[197,2048]{1,0:T(8,128)(4,1)} %get-tuple-element.150, u8[197,2048]{1,0:T(8,128)(4,1)} %get-tuple-element.151), kind=kOutput, calls=%fused_computation.601 | convolution fusion | flops 1709443072 | bytes 9035776 | tf_op jit(solution)/shard_map/blf,fd->bld/dot_general | solution.py:156
  763.2 22.6 %all-reduce.24.cloned.1.call-done = bf16[2,197,1024]{2,1,0:T(8,128)(2,1)} async-done(((bf16[2,197,1024]{2,1,0:T(8,128)(2,1)}), bf16[2,197,1024]{2,1,0:T(8,128)(2,1)}) %all-reduce.24.cloned.1.call-update) | async-done | bytes 806928 | tf_op jit(solution)/shard_map/psum | solution.py:65
  842.4 7.8 copy.283
  855.4 11.3 fusion.169
  866.8 9.1 fusion.167
  875.9 10.6 fusion.100
  886.5 20.6 %copy.287 = bf16[1,2048,1024]{1,0,2:T(2,128)(2,1)} copy(bf16[1,2048,1024]{2,1,0:T(8,128)(2,1)} %fusion.100) | data formatting | bytes 8388608
  907.1 8.0 copy.409
  920.4 5.9 fusion.511
  926.3 8.0 fusion.99
  949.5 38.2 %all-reduce = f32[8,1152]{1,0:T(8,128)S(1)} all-reduce(f32[8,1152]{1,0:T(8,128)S(1)} %constant_dynamic-update-slice_fusion), channel_id=3, replica_groups=mesh['section'=2,'dp'=8,'mp'=2] {'dp'}, use_global_device_ids=true, to_apply=%region_84.85.clone | all-reduce | flops 9216 | bytes 73728
  993.0 19.8 %reduce-scatter.13.cloned.1.call-done = bf16[128,1536]{1,0:T(8,128)(2,1)} async-done(((bf16[1024,1536]{1,0:T(8,128)(2,1)}), bf16[128,1536]{1,0:T(8,128)(2,1)}) %reduce-scatter.13.cloned.1.call-update) | async-done | bytes 393232
  1015.9 87.8 %reduce-scatter.17.cloned.1.call-done = bf16[128,2048]{1,0:T(8,128)(2,1)} async-done(((bf16[1024,2048]{1,0:T(8,128)(2,1)}), bf16[128,2048]{1,0:T(8,128)(2,1)}) %reduce-scatter.17.cloned.1.call-update) | async-done | bytes 524304
  1107.3 87.8 %reduce-scatter.11.cloned.1.call-done = bf16[1,128,2048]{2,1,0:T(8,128)(2,1)} async-done(((bf16[1,1024,2048]{2,1,0:T(8,128)(2,1)}), bf16[1,128,2048]{2,1,0:T(8,128)(2,1)}) %reduce-scatter.11.cloned.1.call-update) | async-done | bytes 524304 | tf_op jit(solution)/shard_map/reduce_scatter | solution.py:58
  (660 shorter events, 302.9 us)
Async XLA Ops:
  7.2 65.9 %all-gather.7.cloned.1.call-start = ((), (), s32[]{:S(2)}) async-start(), calls=%async_computation.4 | async-start | bytes 3538944 | tf_op jit(solution)/shard_map/all_gather | solution.py:24
  7.9 105.3 %all-gather.9.cloned.1.call-start = ((), (), s32[]{:S(2)}) async-start(), calls=%async_computation.5 | async-start | bytes 1179648 | tf_op jit(solution)/shard_map/all_gather | solution.py:24
  8.7 141.6 %all-reduce.14.cloned.1.call-start = ((), (), s32[]{:S(2)}) async-start(), calls=%async_computation.6 | async-start | bytes 1638400 | tf_op jit(solution)/shard_map/psum | solution.py:65
  48.5 176.6 %copy-start.148 = (f32[1024]{0:T(1024)}, f32[1024]{0:T(1024)S(1)}, u32[]{:S(2)}) copy-start(f32[1024]{0:T(1024)S(1)} %get-tuple-element.190) | copy-start | bytes 12292
  48.5 298.2 %copy-start.112 = (f32[1024]{0:T(1024)}, f32[1024]{0:T(1024)S(1)}, u32[]{:S(2)}) copy-start(f32[1024]{0:T(1024)S(1)} %get-tuple-element.189) | copy-start | bytes 12292
  48.5 306.4 %copy-start.152 = (f32[1024]{0:T(1024)}, f32[1024]{0:T(1024)S(1)}, u32[]{:S(2)}) copy-start(f32[1024]{0:T(1024)S(1)} %get-tuple-element.194) | copy-start | bytes 12292
  48.5 556.9 %copy-start.103 = (f32[1024]{0:T(1024)}, f32[1024]{0:T(1024)S(1)}, u32[]{:S(2)}) copy-start(f32[1024]{0:T(1024)S(1)} %get-tuple-element.192) | copy-start | bytes 12292
  51.0 302.0 %copy-start.66 = (bf16[1,2,197,1024]{3,1,2,0:T(2,128)(2,1)}, bf16[1,2,197,1024]{3,1,2,0:T(2,128)(2,1)S(1)}, u32[]{:S(2)}) copy-start(bf16[1,2,197,1024]{3,1,2,0:T(2,128)(2,1)S(1)} %get-tuple-element.173) | copy-start | bytes 2420740
  52.1 306.7 %copy-start.110 = (f32[8,64]{1,0:T(8,128)}, f32[8,64]{1,0:T(8,128)S(1)}, u32[]{:S(2)}) copy-start(f32[8,64]{1,0:T(8,128)S(1)} %add.600) | copy-start | bytes 6148
  52.2 309.4 %copy-start.108 = (f32[8,64]{1,0:T(8,128)}, f32[8,64]{1,0:T(8,128)S(1)}, u32[]{:S(2)}) copy-start(f32[8,64]{1,0:T(8,128)S(1)} %add.603) | copy-start | bytes 6148
  116.0 109.1 %all-gather.11.cloned.1.call-start = ((), (), s32[]{:S(2)}) async-start(), calls=%async_computation.7 | async-start | bytes 4718592 | tf_op jit(solution)/shard_map/all_gather | solution.py:24
  116.6 183.6 %all-gather.13.cloned.1.call-start = ((), (), s32[]{:S(2)}) async-start(), calls=%async_computation.8 | async-start | bytes 4718592 | tf_op jit(solution)/shard_map/all_gather | solution.py:24
  117.2 229.5 %all-reduce.16.cloned.1.call-start = ((), (), s32[]{:S(2)}) async-start(), calls=%async_computation.9 | async-start | bytes 1638400 | tf_op jit(solution)/shard_map/psum | solution.py:65
  118.3 114.0 %copy-start.160 = (f32[2048]{0:T(1024)}, f32[2048]{0:T(1024)S(1)}, u32[]{:S(2)}) copy-start(f32[2048]{0:T(1024)S(1)} %reshape.797) | copy-start | bytes 24580
  150.3 74.8 %copy-start.15 = (bf16[2,197,1024]{2,1,0:T(8,128)(2,1)S(1)}, bf16[2,197,1024]{2,1,0:T(8,128)(2,1)}, u32[]{:S(2)}) copy-start(bf16[2,197,1024]{2,1,0:T(8,128)(2,1)} %all-reduce.14.cloned.1.call-done) | copy-start | bytes 2420740
  313.3 90.8 %all-reduce.18.cloned.1.call-start = ((), (), s32[]{:S(2)}) async-start(), calls=%async_computation.10 | async-start | bytes 1638400 | tf_op jit(solution)/shard_map/psum | solution.py:65
  349.3 3.6 collective-permute-start
  368.8 119.8 %all-reduce.30.cloned.1.call-start = ((), (), s32[]{:S(2)}) async-start(), calls=%async_computation.20 | async-start | bytes 3276800 | tf_op jit(solution)/shard_map/psum | solution.py:65
  369.7 121.6 %copy-start.167 = (f32[2]{0:T(128)}, f32[2]{0:T(128)S(1)}, u32[]{:S(2)}) copy-start(f32[2]{0:T(128)S(1)} %broadcast_select_fusion.29) | copy-start | bytes 28
  409.1 82.2 %copy-start.6 = (f32[2,197,1024]{2,1,0:T(8,128)}, f32[2,197,1024]{2,1,0:T(8,128)S(1)}, u32[]{:S(2)}) copy-start(f32[2,197,1024]{2,1,0:T(8,128)S(1)} %get-tuple-element.145) | copy-start | bytes 4841476
  435.5 159.2 %all-reduce.28.cloned.1.call-start = ((), (), s32[]{:S(2)}) async-start(), calls=%async_computation.19 | async-start | bytes 3276800 | tf_op jit(solution)/shard_map/psum | solution.py:65
  507.3 16.0 %collective-permute-start.1 = (bf16[2,197,1024]{2,0,1:T(2,128)(2,1)}, bf16[2,197,1024]{2,0,1:T(2,128)(2,1)}, u32[]{:S(2)}, u32[]{:S(2)}) collective-permute-start(bf16[2,197,1024]{2,0,1:T(2,128)(2,1)} %copy.214), channel_id=1, source_target_pairs={{0,16},{1,17},{2,18},{3,19},{4,20},{5,21},{6,22},{7,23},{8,24},{9,... | collective-permute-start | bytes 2420744 | tf_op jit(solution)/shard_map/ppermute | solution.py:71
  541.5 119.7 %all-reduce.20.cloned.1.call-start = ((), (), s32[]{:S(2)}) async-start(), calls=%async_computation.11 | async-start | bytes 1638400 | tf_op jit(solution)/shard_map/psum | solution.py:65
  603.8 11.8 collective-permute-start.2
  626.0 102.7 %all-reduce.22.cloned.1.call-start = ((), (), s32[]{:S(2)}) async-start(), calls=%async_computation.12 | async-start | bytes 1638400 | tf_op jit(solution)/shard_map/psum | solution.py:65
  693.5 92.3 %all-reduce.24.cloned.1.call-start = ((), (), s32[]{:S(2)}) async-start(), calls=%async_computation.13 | async-start | bytes 1638400 | tf_op jit(solution)/shard_map/psum | solution.py:65
  735.0 4.8 collective-permute-start.3
  749.7 187.3 %all-reduce.26.cloned.1.call-start = ((), (), s32[]{:S(2)}) async-start(), calls=%async_computation.18 | async-start | bytes 3276800 | tf_op jit(solution)/shard_map/psum | solution.py:65
  813.5 177.6 %reduce-scatter.15.cloned.1.call-start = ((), (), s32[]{:S(2)}) async-start(), calls=%async_computation.16 | async-start | bytes 1179648
  832.1 180.8 %reduce-scatter.13.cloned.1.call-start = ((), (), s32[]{:S(2)}) async-start(), calls=%async_computation.15 | async-start | bytes 3538944
  855.3 248.5 %reduce-scatter.17.cloned.1.call-start = ((), (), s32[]{:S(2)}) async-start(), calls=%async_computation.17 | async-start | bytes 4718592
  915.1 280.0 %reduce-scatter.11.cloned.1.call-start = ((), (), s32[]{:S(2)}) async-start(), calls=%async_computation.14 | async-start | bytes 4718592 | tf_op jit(solution)/shard_map/reduce_scatter | solution.py:58
  (179 other events, 1286.9 us)
Sparse Core Ops, SparseCore 0:
  10.2 62.8 all-gather.6
  75.1 38.0 all-gather.8
  116.1 34.0 all-reduce.13
  152.2 72.7 all-gather.10
  227.0 73.1 all-gather.12
  313.4 33.2 all-reduce.15
  369.0 35.1 all-reduce.17
  435.6 52.9 all-reduce.29
  541.7 52.9 all-reduce.27
  626.1 35.0 all-reduce.19
  693.6 35.0 all-reduce.21
  749.8 35.9 all-reduce.23
  813.7 52.9 all-reduce.25
  870.5 64.1 reduce-scatter.14
  938.2 74.6 reduce-scatter.12
  1016.3 87.3 reduce-scatter.16
  1107.2 87.9 reduce-scatter.10
where the time goes:
time: 1210 us; the launch traced here: 1200 us
  waiting for transfers between devices  669 us (55%)
  matrix products  222 us (18%)
  local copies, waits for them, and re-layouts  137 us (11%)
  other arithmetic  78.5 us (6%)
  blocking collectives  71.1 us (6%)
  between operations  16.9 us (1%)
    psum x9, waiting for transfers between devices, both_halves(): return lax.psum(partial.astype(jnp.bfloat16), 'mp').astype(jnp.float32)  283 us
    all_gather x4, waiting for transfers between devices, gather_all(): lax.all_gather(piece, 'dp', axis=axis, tiled=True)  186 us
    unnamed x20, waiting for transfers between devices  110 us
    reduce_scatter x1, waiting for transfers between devices, scatter_all(): lax.psum_scatter(totals[index].astype(jnp.bfloat16), 'dp', scatter_dimens...  87.8 us
    unnamed x407, local copies, waits for them, and re-layouts  79.7 us
    unnamed x1, blocking collectives  38.2 us
    dot_general x3, matrix products, forward(): jnp.einsum('blf,fd->bld', gelu_out, down_mat, preferred_element_type=jnp....  37.7 us
    all_gather x1, blocking collectives, gather_all(): packed = lax.all_gather(flat, 'dp', axis=0, tiled=False)  32.9 us
  transfers between devices with their start and end apart: 21, of which 16 were waited for; matrix products, arithmetic and copies ran while one was open for 20% of the time, Pallas kernels for 0%

commit v1 on v0

--- a/solution.py
+++ b/solution.py
@@ -3,9 +3,15 @@
 import jax.numpy as jnp
 from jax import lax
 from jax.sharding import PartitionSpec as P
+from jax.lax import all_gather
 
 HD = 64
 epsilon = 1e-06
+
+
+def launch_rounds_up(in_array, a_name="mp"):
+    local_part = jnp.sum(all_gather(in_array, axis_name=a_name), axis=0)
+    return local_part
 
 
 def gather_all(small, big):
@@ -62,7 +68,7 @@
 
 
 def both_halves(partial):
-    return lax.psum(partial.astype(jnp.bfloat16), "mp").astype(jnp.float32)
+    return launch_rounds_up(partial.astype(jnp.bfloat16)).astype(jnp.float32)
 
 
 def from_behind(x, axis, by):

time: 1210 us -> 1140 us (0.942)
  waiting for transfers between devices: 669 us -> 540 us
  other arithmetic: 78.5 us -> 115 us
  matrix products: 222 us -> 236 us
    psum x9 -> x0, waiting for transfers between devices: 283 us -> none  [both_halves(): return lax.psum(partial.astype(jnp.bfloat16), 'mp').astype(jnp.float32)]
    all_gather x0 -> x12, waiting for transfers between devices: none -> 187 us  [launch_rounds_up(): local_part = jnp.sum(all_gather(in_array, axis_name=a_name), axis=0)]
    reduce_sum x0 -> x12, other arithmetic: none -> 33.5 us  [launch_rounds_up(): local_part = jnp.sum(all_gather(in_array, axis_name=a_name), axis=0)]
    unnamed x20 -> x23, waiting for transfers between devices: 110 us -> 77.9 us
    unnamed x407 -> x361, local copies, waits for them, and re-layouts: 79.7 us -> 80.3 us
  transfers between devices with their start and end apart: 21 -> 24, of which waited for: 16 -> 18; matrix products, arithmetic and copies ran while one was open for 20% -> 30% of each run, Pallas kernels for 0% -> 0%
where the time goes in v1:
time: 1140 us; the launch traced here: 1130 us
  waiting for transfers between devices  540 us (47%)
  matrix products  236 us (21%)
  local copies, waits for them, and re-layouts  145 us (13%)
  other arithmetic  115 us (10%)
  blocking collectives  71.1 us (6%)
  between operations  16.6 us (1%)
    all_gather x12, waiting for transfers between devices, launch_rounds_up(): local_part = jnp.sum(all_gather(in_array, axis_name=a_name), axis=0)  187 us
    all_gather x4, waiting for transfers between devices, gather_all(): lax.all_gather(piece, 'dp', axis=axis, tiled=True)  185 us
    reduce_scatter x1, waiting for transfers between devices, scatter_all(): lax.psum_scatter(totals[index].astype(jnp.bfloat16), 'dp', scatter_dimens...  87.9 us
    unnamed x361, local copies, waits for them, and re-layouts  80.3 us
    unnamed x23, waiting for transfers between devices  77.9 us
    dot_general x3, matrix products, forward(): jnp.einsum('blf,fd->bld', gelu_out, down_mat, preferred_element_type=jnp....  38.8 us
    unnamed x1, blocking collectives  38.2 us
    reduce_sum x12, other arithmetic, launch_rounds_up(): local_part = jnp.sum(all_gather(in_array, axis_name=a_name), axis=0)  33.5 us
  transfers between devices with their start and end apart: 24, of which 18 were waited for; matrix products, arithmetic and copies ran while one was open for 30% of the time, Pallas kernels for 0%

profile of v1, /device:TPU:0, one launch (start us, length us, event | category | flops | bytes accessed | tf_op | source)
XLA Modules:
  0.0 1133.7 jit_solution(5799825334629804833)
XLA Ops:
  15.5 32.9 %all-gather.13 = bf16[8,1,1152]{2,1,0:T(2,128)(2,1)S(1)} all-gather(bf16[1,1,1152]{2,1,0:T(2,128)(2,1)S(1)} %reshape.826), channel_id=2, replica_groups=mesh['section'=2,'dp'=8,'mp'=2] {'dp'}, dimensions={0}, use_global_device_ids=true | all-gather | bytes 20736 | tf_op jit(solution)/shard_map/all_gather | solution.py:19
  53.3 19.8 %all-gather.31.cloned.1.call-done = bf16[1,3,1024,512]{3,2,1,0:T(8,128)(2,1)} async-done(((bf16[1,3,128,512]{3,2,1,0:T(8,128)(2,1)}), bf16[1,3,1024,512]{3,2,1,0:T(8,128)(2,1)}) %all-gather.31.cloned.1.call-update) | async-done | bytes 3145744 | tf_op jit(solution)/shard_map/all_gather | solution.py:30
  87.2 26.0 %all-gather.33.cloned.1.call-done = bf16[1,512,1024]{2,1,0:T(8,128)(2,1)} async-done(((bf16[1,512,128]{2,1,0:T(8,128)(2,1)}), bf16[1,512,1024]{2,1,0:T(8,128)(2,1)}) %all-gather.33.cloned.1.call-update) | async-done | bytes 1048592 | tf_op jit(solution)/shard_map/all_gather | solution.py:30
  117.6 25.5 %all-gather.39.cloned.1.call-done = bf16[4,197,1024]{2,1,0:T(8,128)(2,1)} async-done(((bf16[2,197,1024]{2,1,0:T(8,128)(2,1)}), bf16[4,197,1024]{2,1,0:T(8,128)(2,1)}) %all-gather.39.cloned.1.call-update) | async-done | bytes 1613840 | tf_op jit(solution)/shard_map/all_gather | solution.py:13
  146.3 71.7 %all-gather.35.cloned.1.call-done = bf16[1,1024,2048]{2,1,0:T(8,128)(2,1)} async-done(((bf16[1,128,2048]{2,1,0:T(8,128)(2,1)}), bf16[1,1024,2048]{2,1,0:T(8,128)(2,1)}) %all-gather.35.cloned.1.call-update) | async-done | bytes 4194320 | tf_op jit(solution)/shard_map/all_gather | solution.py:30
  217.9 7.2 fusion.583
  225.1 67.9 %all-gather.37.cloned.1.call-done = bf16[1,2048,1024]{2,1,0:T(8,128)(2,1)} async-done(((bf16[1,2048,128]{2,1,0:T(8,128)(2,1)}), bf16[1,2048,1024]{2,1,0:T(8,128)(2,1)}) %all-gather.37.cloned.1.call-update) | async-done | bytes 4194320 | tf_op jit(solution)/shard_map/all_gather | solution.py:30
  293.0 13.1 %fusion.466 = bf16[2,197,1024]{2,1,0:T(8,128)(2,1)} fusion(bf16[1,2048,1024]{2,1,0:T(8,128)(2,1)} %all-gather.37.cloned.1.call-done, f32[2,197,2048]{2,1,0:T(8,128)} %get-tuple-element.208, u8[197,2048]{1,0:T(8,128)(4,1)S(1)} %get-tuple-element.89, u8[197,2048]{1,0:T(8,128)(4,1)S(1)} %get-tuple-element.88), kind=kOutput, calls=%fused_computation.606 | convolution fusion | flops 1709443072 | bytes 9035776 | tf_op jit(solution)/shard_map/blf,fd->bld/dot_general | solution.py:162
  307.4 25.0 %all-gather.41.cloned.1.call-done = bf16[4,197,1024]{2,1,0:T(8,128)(2,1)} async-done(((bf16[2,197,1024]{2,1,0:T(8,128)(2,1)}), bf16[4,197,1024]{2,1,0:T(8,128)(2,1)}) %all-gather.41.cloned.1.call-update) | async-done | bytes 1613840 | tf_op jit(solution)/shard_map/all_gather | solution.py:13
  371.1 18.6 %all-gather.43.cloned.1.call-done = bf16[4,197,1024]{2,1,0:T(8,128)(2,1)} async-done(((bf16[2,197,1024]{2,1,0:T(8,128)(2,1)}), bf16[4,197,1024]{2,1,0:T(8,128)(2,1)}) %all-gather.43.cloned.1.call-update) | async-done | bytes 1613840 | tf_op jit(solution)/shard_map/all_gather | solution.py:13
  394.9 8.4 fusion.580
  413.5 12.8 %fusion.471 = bf16[2,197,1024]{2,1,0:T(8,128)(2,1)} fusion(bf16[1,2048,1024]{2,1,0:T(8,128)(2,1)} %all-gather.37.cloned.1.call-done, f32[2,197,2048]{2,1,0:T(8,128)} %get-tuple-element.211, u8[197,2048]{1,0:T(8,128)(4,1)} %get-tuple-element.160, u8[197,2048]{1,0:T(8,128)(4,1)} %get-tuple-element.161), kind=kOutput, calls=%fused_computation.607 | convolution fusion | flops 1709443072 | bytes 9035776 | tf_op jit(solution)/shard_map/blf,fd->bld/dot_general | solution.py:162
  426.8 12.9 %all-gather.51.cloned.1.call-done = bf16[4,197,1024]{2,1,0:T(8,128)(2,1)} async-done(((bf16[2,197,1024]{2,1,0:T(8,128)(2,1)}), bf16[4,197,1024]{2,1,0:T(8,128)(2,1)}) %all-gather.51.cloned.1.call-update) | async-done | bytes 1613840 | tf_op jit(solution)/shard_map/all_gather | solution.py:13
  461.5 8.4 all-gather.45.cloned.1.call-done
  527.1 27.1 %all-gather.47.cloned.1.call-done = bf16[4,197,1024]{2,1,0:T(8,128)(2,1)} async-done(((bf16[2,197,1024]{2,1,0:T(8,128)(2,1)}), bf16[4,197,1024]{2,1,0:T(8,128)(2,1)}) %all-gather.47.cloned.1.call-update) | async-done | bytes 1613840 | tf_op jit(solution)/shard_map/all_gather | solution.py:13
  558.8 5.4 fusion.844
  568.1 10.1 fusion.582
  593.1 23.6 %all-gather.55.cloned.1.call-done = bf16[4,197,1024]{2,1,0:T(8,128)(2,1)} async-done(((bf16[2,197,1024]{2,1,0:T(8,128)(2,1)}), bf16[4,197,1024]{2,1,0:T(8,128)(2,1)}) %all-gather.55.cloned.1.call-update) | async-done | bytes 1613840 | tf_op jit(solution)/shard_map/all_gather | solution.py:13
  652.8 27.2 %all-gather.57.cloned.1.call-done = bf16[4,197,1024]{2,1,0:T(8,128)(2,1)} async-done(((bf16[2,197,1024]{2,1,0:T(8,128)(2,1)}), bf16[4,197,1024]{2,1,0:T(8,128)(2,1)}) %all-gather.57.cloned.1.call-update) | async-done | bytes 1613840 | tf_op jit(solution)/shard_map/all_gather | solution.py:13
  703.1 12.9 %fusion.476 = bf16[2,197,1024]{2,1,0:T(8,128)(2,1)} fusion(bf16[1,2048,1024]{2,1,0:T(8,128)(2,1)} %all-gather.37.cloned.1.call-done, f32[2,197,2048]{2,1,0:T(8,128)} %get-tuple-element.216, u8[197,2048]{1,0:T(8,128)(4,1)} %get-tuple-element.158, u8[197,2048]{1,0:T(8,128)(4,1)} %get-tuple-element.159), kind=kOutput, calls=%fused_computation.608 | convolution fusion | flops 1709443072 | bytes 9035776 | tf_op jit(solution)/shard_map/blf,fd->bld/dot_general | solution.py:162
  716.4 15.5 %all-gather.59.cloned.1.call-done = bf16[4,197,1024]{2,1,0:T(8,128)(2,1)} async-done(((bf16[2,197,1024]{2,1,0:T(8,128)(2,1)}), bf16[4,197,1024]{2,1,0:T(8,128)(2,1)}) %all-gather.59.cloned.1.call-update) | async-done | bytes 1613840 | tf_op jit(solution)/shard_map/all_gather | solution.py:13
  798.0 7.6 copy.391
  810.9 11.6 %fusion.169 = f32[2048,1024,1]{1,0,2:T(8,128)S(1)} fusion(f32[2,197,2048]{2,1,0:T(8,128)} %copy-done.163, u8[197,2048]{1,0:T(8,128)(4,1)S(1)} %copy-done.166, f32[2]{0:T(128)S(1)} %copy-done.147, bf16[1,2,197,1024]{3,1,2,0:T(2,128)(2,1)S(1)} %copy-done.72, pred[]{:T(512)S(6)} %eq.3), kind=kOutput, calls=%fused_computation.286 | convolution fusion | flops 1709039616 | bytes 12826633 | tf_op jit(solution)/shard_map/blf,bld->fd/dot_general | solution.py:192
  822.5 9.1 fusion.167
  831.6 10.6 fusion.100
  842.2 20.6 %copy.395 = bf16[1,2048,1024]{1,0,2:T(2,128)(2,1)} copy(bf16[1,2048,1024]{2,1,0:T(8,128)(2,1)} %fusion.100) | data formatting | bytes 8388608
  862.8 8.0 copy.517
  876.2 5.9 fusion.520
  882.0 8.0 fusion.99
  911.3 38.2 %all-reduce = f32[8,1152]{1,0:T(8,128)S(1)} all-reduce(f32[8,1152]{1,0:T(8,128)S(1)} %constant_dynamic-update-slice_fusion), channel_id=15, replica_groups=mesh['section'=2,'dp'=8,'mp'=2] {'dp'}, use_global_device_ids=true, to_apply=%region_84.85.clone | all-reduce | flops 9216 | bytes 73728
  957.9 75.2 %reduce-scatter.17.cloned.1.call-done = bf16[128,2048]{1,0:T(8,128)(2,1)} async-done(((bf16[1024,2048]{1,0:T(8,128)(2,1)}), bf16[128,2048]{1,0:T(8,128)(2,1)}) %reduce-scatter.17.cloned.1.call-update) | async-done | bytes 524304
  1036.7 87.9 %reduce-scatter.11.cloned.1.call-done = bf16[1,128,2048]{2,1,0:T(8,128)(2,1)} async-done(((bf16[1,1024,2048]{2,1,0:T(8,128)(2,1)}), bf16[1,128,2048]{2,1,0:T(8,128)(2,1)}) %reduce-scatter.11.cloned.1.call-update) | async-done | bytes 524304 | tf_op jit(solution)/shard_map/reduce_scatter | solution.py:64
  (635 shorter events, 362.6 us)
Async XLA Ops:
  7.2 65.9 %all-gather.31.cloned.1.call-start = ((), (), s32[]{:S(2)}) async-start(), calls=%async_computation.4 | async-start | bytes 3538944 | tf_op jit(solution)/shard_map/all_gather | solution.py:30
  7.9 105.3 %all-gather.33.cloned.1.call-start = ((), (), s32[]{:S(2)}) async-start(), calls=%async_computation.5 | async-start | bytes 1179648 | tf_op jit(solution)/shard_map/all_gather | solution.py:30
  8.7 134.5 %all-gather.39.cloned.1.call-start = ((), (), s32[]{:S(2)}) async-start(), calls=%async_computation.9 | async-start | bytes 2457600 | tf_op jit(solution)/shard_map/all_gather | solution.py:13
  49.0 519.0 %copy-start.95 = (f32[1024]{0:T(1024)}, f32[1024]{0:T(1024)S(1)}, u32[]{:S(2)}) copy-start(f32[1024]{0:T(1024)S(1)} %get-tuple-element.200) | copy-start | bytes 12292
  51.5 290.1 %copy-start.64 = (bf16[1,2,197,1024]{3,1,2,0:T(2,128)(2,1)}, bf16[1,2,197,1024]{3,1,2,0:T(2,128)(2,1)S(1)}, u32[]{:S(2)}) copy-start(bf16[1,2,197,1024]{3,1,2,0:T(2,128)(2,1)S(1)} %get-tuple-element.181) | copy-start | bytes 2420740
  87.2 55.9 %copy-start.75 = (bf16[2,8,64,197]{3,2,1,0:T(8,128)(2,1)}, bf16[2,8,64,197]{3,2,1,0:T(8,128)(2,1)S(1)}, u32[]{:S(2)}) copy-start(bf16[2,8,64,197]{3,2,1,0:T(8,128)(2,1)S(1)} %fusion.490) | copy-start | bytes 1210372
  116.0 101.9 %all-gather.35.cloned.1.call-start = ((), (), s32[]{:S(2)}) async-start(), calls=%async_computation.6 | async-start | bytes 4718592 | tf_op jit(solution)/shard_map/all_gather | solution.py:30
  116.6 101.3 %copy-start.134 = (f32[1024]{0:T(1024)S(1)}, f32[1024]{0:T(1024)}, u32[]{:S(2)}) copy-start(f32[1024]{0:T(1024)} %get-tuple-element.198) | copy-start | bytes 12292
  116.6 176.4 %all-gather.37.cloned.1.call-start = ((), (), s32[]{:S(2)}) async-start(), calls=%async_computation.7 | async-start | bytes 4718592 | tf_op jit(solution)/shard_map/all_gather | solution.py:30
  117.2 215.2 %all-gather.41.cloned.1.call-start = ((), (), s32[]{:S(2)}) async-start(), calls=%async_computation.10 | async-start | bytes 2457600 | tf_op jit(solution)/shard_map/all_gather | solution.py:13
  306.1 83.6 %all-gather.43.cloned.1.call-start = ((), (), s32[]{:S(2)}) async-start(), calls=%async_computation.11 | async-start | bytes 2457600 | tf_op jit(solution)/shard_map/all_gather | solution.py:13
  338.0 3.6 collective-permute-start
  361.6 78.2 %all-gather.51.cloned.1.call-start = ((), (), s32[]{:S(2)}) async-start(), calls=%async_computation.15 | async-start | bytes 2457600 | tf_op jit(solution)/shard_map/all_gather | solution.py:13
  362.5 83.5 %copy-start.146 = (f32[2]{0:T(128)}, f32[2]{0:T(128)S(1)}, u32[]{:S(2)}) copy-start(f32[2]{0:T(128)S(1)} %broadcast_select_fusion.27) | copy-start | bytes 28
  391.8 81.0 %copy-start.17 = (bf16[2,197,1024]{2,1,0:T(8,128)(2,1)}, bf16[2,197,1024]{2,1,0:T(8,128)(2,1)S(1)}, u32[]{:S(2)}) copy-start(bf16[2,197,1024]{2,1,0:T(8,128)(2,1)S(1)} %reduce_sum.775) | copy-start | bytes 2420740
  411.7 58.2 %all-gather.45.cloned.1.call-start = ((), (), s32[]{:S(2)}) async-start(), calls=%async_computation.12 | async-start | bytes 2457600 | tf_op jit(solution)/shard_map/all_gather | solution.py:13
  426.4 97.8 %all-gather.53.cloned.1.call-start = ((), (), s32[]{:S(2)}) async-start(), calls=%async_computation.16 | async-start | bytes 2457600 | tf_op jit(solution)/shard_map/all_gather | solution.py:13
  477.8 18.5 %collective-permute-start.1 = (bf16[2,197,1024]{2,0,1:T(2,128)(2,1)}, bf16[2,197,1024]{2,0,1:T(2,128)(2,1)}, u32[]{:S(2)}, u32[]{:S(2)}) collective-permute-start(bf16[2,197,1024]{2,0,1:T(2,128)(2,1)} %copy.322), channel_id=1, source_target_pairs={{0,16},{1,17},{2,18},{3,19},{4,20},{5,21},{6,22},{7,23},{8,24},{9,... | collective-permute-start | bytes 2420744 | tf_op jit(solution)/shard_map/ppermute | solution.py:77
  496.1 58.2 %all-gather.47.cloned.1.call-start = ((), (), s32[]{:S(2)}) async-start(), calls=%async_computation.13 | async-start | bytes 2457600 | tf_op jit(solution)/shard_map/all_gather | solution.py:13
  519.5 97.1 %all-gather.55.cloned.1.call-start = ((), (), s32[]{:S(2)}) async-start(), calls=%async_computation.17 | async-start | bytes 2457600 | tf_op jit(solution)/shard_map/all_gather | solution.py:13
  520.9 43.2 %copy-start.113 = (f32[2,197]{1,0:T(2,128)}, f32[2,197]{1,0:T(2,128)S(1)}, u32[]{:S(2)}) copy-start(f32[2,197]{1,0:T(2,128)S(1)} %add_rsqrt_fusion.4) | copy-start | bytes 4732
  566.3 11.9 %collective-permute-start.2 = (bf16[2,197,1024]{2,0,1:T(2,128)(2,1)S(1)}, bf16[2,197,1024]{2,0,1:T(2,128)(2,1)S(1)}, u32[]{:S(2)}, u32[]{:S(2)}) collective-permute-start(bf16[2,197,1024]{2,0,1:T(2,128)(2,1)S(1)} %copy.337), channel_id=1, source_target_pairs={{16,0},{17,1},{18,2},{19,3},{20,4},{21,5},{22,6},{23,7},{24,8},{25... | collective-permute-start | bytes 2420744 | tf_op jit(solution)/shard_map/ppermute | solution.py:77
  588.6 91.4 %all-gather.57.cloned.1.call-start = ((), (), s32[]{:S(2)}) async-start(), calls=%async_computation.18 | async-start | bytes 2457600 | tf_op jit(solution)/shard_map/all_gather | solution.py:13
  651.9 80.0 %all-gather.59.cloned.1.call-start = ((), (), s32[]{:S(2)}) async-start(), calls=%async_computation.19 | async-start | bytes 2457600 | tf_op jit(solution)/shard_map/all_gather | solution.py:13
  652.8 35.5 %copy-start.111 = (f32[2,197]{1,0:T(2,128)}, f32[2,197]{1,0:T(2,128)S(1)}, u32[]{:S(2)}) copy-start(f32[2,197]{1,0:T(2,128)S(1)} %add_rsqrt_fusion.2) | copy-start | bytes 4732
  689.2 4.2 collective-permute-start.3
  703.0 189.1 %all-gather.49.cloned.1.call-start = ((), (), s32[]{:S(2)}) async-start(), calls=%async_computation.14 | async-start | bytes 2457600 | tf_op jit(solution)/shard_map/all_gather | solution.py:13
  716.0 179.8 %all-gather.61.cloned.1.call-start = ((), (), s32[]{:S(2)}) async-start(), calls=%async_computation.20 | async-start | bytes 2457600 | tf_op jit(solution)/shard_map/all_gather | solution.py:13
  769.1 183.8 %reduce-scatter.15.cloned.1.call-start = ((), (), s32[]{:S(2)}) async-start(), calls=%async_computation.22 | async-start | bytes 1179648
  787.9 166.9 %reduce-scatter.13.cloned.1.call-start = ((), (), s32[]{:S(2)}) async-start(), calls=%async_computation.21 | async-start | bytes 3538944
  810.8 222.3 %reduce-scatter.17.cloned.1.call-start = ((), (), s32[]{:S(2)}) async-start(), calls=%async_computation.23 | async-start | bytes 4718592
  870.9 253.7 %reduce-scatter.11.cloned.1.call-start = ((), (), s32[]{:S(2)}) async-start(), calls=%async_computation.8 | async-start | bytes 4718592 | tf_op jit(solution)/shard_map/reduce_scatter | solution.py:64
  (159 other events, 891.6 us)
Sparse Core Ops, SparseCore 0:
  10.2 62.8 all-gather.30
  75.1 38.1 all-gather.32
  116.1 26.9 all-gather.38
  145.1 72.7 all-gather.34
  219.8 73.1 all-gather.36
  306.3 26.1 all-gather.40
  361.7 27.9 all-gather.42
  411.8 27.9 all-gather.50
  441.9 27.9 all-gather.44
  496.2 27.9 all-gather.52
  526.3 27.9 all-gather.46
  588.7 27.9 all-gather.54
  652.0 27.9 all-gather.56
  703.1 28.7 all-gather.58
  733.3 27.9 all-gather.48
  769.2 27.8 all-gather.60
  800.9 64.0 reduce-scatter.14
  868.4 73.5 reduce-scatter.12
  945.6 87.4 reduce-scatter.16
  1036.6 87.9 reduce-scatter.10
